TPU v7x, 512 devices: a whole 4x4x16 slice. The times are simulated.
512 devices in a mesh: box: 16 (over x, y_hi, core), sib: 2 (over y_lo), grp: 16 (over z).
Axes of the slice: x: 4, y: 4 (y_hi: 2, y_lo: 2; y = y_hi * 2 + y_lo), z: 16, core: 2. Of those that a mesh axis runs over, the one named last changes fastest.
Arguments:
- interface_maps: float32 [2, 32, 1024, 1024], P('sib', 'box', 'grp'), parts along dimension 1, may hold values from -1 to 1
- pivot_inverses: float32 [2, 32, 512, 512], P('sib', 'box', None, 'grp'), parts along dimension 1, may hold values from -1 to 5
- exterior_coupling: float32 [32, 1024, 5120], P('box', 'sib', 'grp'), parts along dimension 0, may hold values from -1 to 1
- face_blocks: int32 [32, 8], P('box'), parts along dimension 0, may hold values from 0 to 7, each once within a row
Outputs:
- interface_schur: float32 [32, 1024, 1024], P('box', 'sib', 'grp'), parts along dimension 0
- exterior_update: float32 [32, 1024, 5120], P('box', 'sib', 'grp'), parts along dimension 0
- multipliers: float32 [32, 1024, 1024], P('box', 'grp', 'sib'), parts along dimension 0
There are 16 independent parts, one for each index of `box`. A program takes and returns all parts, laid end to end along the dimension named above; each array names one. Nothing has to cross between parts.
Inputs may be any that keep to these rules, and one draw needn't show every extreme that they name: `face_blocks`: each row is an ordering of the 8 blocks of one child: row 0 for the first child, row 1 for the second.
All inputs are finite; a program needn't handle non-finite values.
Results may differ from a plain program's by a relative error of at most 0.0001.
Values sent between devices are 32-bit elements; how exact they have to be, the bound alone decides.
A program may use at most 128 MiB of HBM per device.

v0:
```python
import jax
import jax.numpy as jnp
from jax import lax
from jax.sharding import PartitionSpec as P


def partner(block, axis, bit):
    count = lax.axis_size(axis)
    route = []
    for low in range(count):
        high = low | 1 << bit
        if high != low and high < count:
            route += [(low, high), (high, low)]
    return lax.ppermute(block, axis, route)


def in_blocks(shard, dim, count):
    dims = shard.shape
    pieces = shard.reshape(*dims[:dim], count, dims[dim] // count, *dims[dim + 1 :])
    return jnp.moveaxis(pieces, dim, 0)


def summed_on_arrival(shard, axis, dim):
    pieces = in_blocks(shard, dim, lax.axis_size(axis))
    arrived = lax.all_to_all(pieces, axis, split_axis=0, concat_axis=0, tiled=True)
    return arrived.sum(axis=0)


def in_one_piece(arrays, axis, dim, along):
    ends, at = ([], 0)
    for a in arrays[:-1]:
        at += a.shape[along]
        ends.append(at)
    both = jnp.concatenate(arrays, axis=along)
    return tuple(jnp.split(summed_on_arrival(both, axis, dim), ends, axis=along))


def complex_dot(left_side, right_side):

    def product(first_part, second_part):
        return jnp.dot(
            first_part,
            second_part,
            precision=lax.Precision.HIGHEST,
            preferred_element_type=jnp.float32,
        )

    real_part = product(left_side[0], right_side[0]) - product(left_side[1], right_side[1])
    imag_part = product(left_side[0], right_side[1]) + product(left_side[1], right_side[0])
    return jnp.stack([real_part, imag_part])


def block_sources(face_blocks):
    alpha_order = face_blocks[0]
    beta_order = face_blocks[1]
    slots = jnp.arange(face_blocks.shape[1], dtype=jnp.int32)
    beta_match = (beta_order[:, None] == slots[None, :]).astype(jnp.int32)
    alpha_match = (alpha_order[:, None] == slots[None, :]).astype(jnp.int32)
    to_beta = jnp.sum(beta_match * alpha_order[:, None], axis=0)
    to_alpha = jnp.sum(alpha_match * beta_order[:, None], axis=0)
    return (to_beta, to_alpha)


def reorder(matrix, source):
    blocks = source.shape[0]
    grouped = matrix.reshape(matrix.shape[0], blocks, matrix.shape[1] // blocks, matrix.shape[2])
    return jnp.take(grouped, source, axis=1).reshape(matrix.shape)


def per_device(interface_maps, pivot_inverses, exterior_coupling, face_blocks):
    own_rows = interface_maps[0]
    partner_rows = partner(own_rows, "sib", 0)
    sibling = lax.axis_index("sib")
    member = lax.axis_index("grp")
    alpha_rows = jnp.where(sibling == 0, own_rows, partner_rows)
    beta_rows = jnp.where(sibling == 0, partner_rows, own_rows)
    local_rows = own_rows.shape[1]
    order_size = own_rows.shape[2]
    panel_width = pivot_inverses.shape[2]
    half_rows = order_size // 2
    to_beta, to_alpha = block_sources(face_blocks)
    panel_section = lax.dynamic_slice_in_dim(alpha_rows, sibling * panel_width, panel_width, 2)
    raw_multipliers = complex_dot(
        panel_section, lax.all_gather(pivot_inverses, "grp", axis=3, tiled=True)[0]
    )
    beta_cols = lax.all_to_all(beta_rows, "grp", split_axis=2, concat_axis=1, tiled=True)
    beta_perm = reorder(beta_cols, to_alpha)
    local_cols = beta_perm.shape[2]
    beta_panel = lax.dynamic_slice_in_dim(beta_perm, sibling * panel_width, panel_width, 1)
    piece = lax.all_gather(raw_multipliers, "grp", axis=1, tiled=True)
    joined = jnp.concatenate(
        [piece, -complex_dot(piece, beta_panel), complex_dot(piece, exterior_coupling)], axis=2
    )
    joined = reorder(joined, to_beta)
    multipliers = lax.dynamic_slice_in_dim(
        joined[:, :, :panel_width], member * local_rows, local_rows, 1
    )
    partial_schur = joined[:, :, panel_width : panel_width + local_cols]
    partial_exterior = joined[:, :, panel_width + local_cols :]
    summed_schur, exterior_update = in_one_piece((partial_schur, partial_exterior), "sib", 1, 2)
    row_index = sibling * half_rows + jnp.arange(half_rows, dtype=jnp.int32)
    col_index = member * local_cols + jnp.arange(local_cols, dtype=jnp.int32)
    identity_real = (row_index[:, None] == col_index[None, :]).astype(jnp.float32)
    identity_block = jnp.stack([identity_real, jnp.zeros_like(identity_real)])
    interface_schur = identity_block + summed_schur
    return (interface_schur, exterior_update, multipliers)


def solution(mesh):
    in_specs = (
        P("sib", "box", "grp", None),
        P("sib", "box", None, "grp"),
        P("box", "sib", "grp"),
        P("box", None),
    )
    out_specs = (P("box", "sib", "grp"), P("box", "sib", "grp"), P("box", "grp", "sib"))
    return jax.shard_map(
        per_device, mesh=mesh, in_specs=in_specs, out_specs=out_specs, check_vma=False
    )
```

profile of v0, /device:TPU:4, one launch (start us, length us, event | category | flops | bytes accessed | tf_op | source)
XLA Modules:
  0.0 277.3 jit_solution(12519139690456995614)
XLA Ops:
  7.9 3.5 %collective-permute-start = (f32[2,64,1024]{2,1,0:T(8,128)}, f32[2,64,1024]{2,1,0:T(8,128)S(1)}, u32[]{:S(2)}, u32[]{:S(2)}) collective-permute-start(f32[2,64,1024]{2,1,0:T(8,128)} %bitcast.121), channel_id=1, source_target_pairs={{0,16},{16,0},{1,17},{17,1},{2,18},{18,2},{3,19},{19,3},{4,20},{20... | collective-permute-start | bytes 1572872 | tf_op jit(solution)/shard_map/ppermute | solution.py:14
  11.4 12.3 %collective-permute-done = f32[2,64,1024]{2,1,0:T(8,128)S(1)} collective-permute-done((f32[2,64,1024]{2,1,0:T(8,128)}, f32[2,64,1024]{2,1,0:T(8,128)S(1)}, u32[]{:S(2)}, u32[]{:S(2)}) %collective-permute-start) | collective-permute-done | bytes 524320 | tf_op jit(solution)/shard_map/ppermute | solution.py:14
  24.7 62.4 %all-gather.3.cloned.1.call-done = f32[1,2,512,512]{2,3,1,0:T(8,128)} async-done(((f32[1,2,512,32]{2,3,1,0:T(8,128)}), f32[1,2,512,512]{2,3,1,0:T(8,128)}) %all-gather.3.cloned.1.call-update) | async-done | bytes 2097168 | tf_op jit(solution)/shard_map/all_gather | solution.py:84
  87.1 2.5 fusion.19
  89.6 2.3 fusion.18
  97.5 8.0 %all-to-all-start = ((f32[16,1,8192]{2,1,0:T(1,128)}), f32[16,1,8192]{2,1,0:T(1,128)S(1)}, u32[]{:S(2)}, u32[]{:S(2)}) async-start(f32[16,1,8192]{2,1,0:T(1,128)} %reshape.137), calls=%async_computation | async-start | bytes 1048576 | tf_op jit(solution)/shard_map/all_to_all | solution.py:86
  105.9 24.2 %all-to-all-done = f32[16,1,8192]{2,1,0:T(1,128)S(1)} async-done(((f32[16,1,8192]{2,1,0:T(1,128)}), f32[16,1,8192]{2,1,0:T(1,128)S(1)}, u32[]{:S(2)}, u32[]{:S(2)}) %all-to-all-start) | async-done | bytes 524320 | tf_op jit(solution)/shard_map/all_to_all | solution.py:86
  134.8 43.9 %all-gather.5.cloned.1.call-done = f32[2,1024,512]{2,1,0:T(8,128)} async-done(((f32[2,64,512]{2,1,0:T(8,128)}), f32[2,1024,512]{2,1,0:T(8,128)}) %all-gather.5.cloned.1.call-update) | async-done | bytes 4194320 | tf_op jit(solution)/shard_map/all_gather | solution.py:90
  178.7 3.9 %fusion.3 = f32[1024,64]{0,1:T(8,128)S(1)} fusion(f32[2,1024,512]{2,1,0:T(8,128)} %all-gather.5.cloned.1.call-done, f32[2,512,64]{1,2,0:T(8,128)S(1)} %dynamic-slice_select_fusion), kind=kOutput, calls=%fused_computation.10 | convolution fusion | flops 402653184 | bytes 2490368 | tf_op jit(solution)/shard_map/dot_general | solution.py:41
  182.6 3.7 %fusion.2 = f32[1024,64]{0,1:T(8,128)S(1)} fusion(f32[2,1024,512]{2,1,0:T(8,128)} %all-gather.5.cloned.1.call-done, f32[2,512,64]{1,2,0:T(8,128)S(1)} %dynamic-slice_select_fusion), kind=kOutput, calls=%fused_computation.9 | convolution fusion | flops 402653184 | bytes 2490368 | tf_op jit(solution)/shard_map/dot_general | solution.py:41
  186.3 2.2 fusion.13
  188.5 2.2 fusion.15
  192.0 4.3 %fusion.1 = f32[1024,320]{0,1:T(8,128)S(1)} fusion(f32[2,1024,512]{2,1,0:T(8,128)} %all-gather.5.cloned.1.call-done, f32[2,512,320]{1,2,0:T(8,128)S(1)} %copy-done.4), kind=kOutput, calls=%fused_computation.8 | convolution fusion | flops 2013265920 | bytes 4063232 | tf_op jit(solution)/shard_map/dot_general | solution.py:41
  196.3 3.9 %fusion = f32[1024,320]{0,1:T(8,128)S(1)} fusion(f32[2,1024,512]{2,1,0:T(8,128)} %all-gather.5.cloned.1.call-done, f32[2,512,320]{1,2,0:T(8,128)S(1)} %copy-done.4), kind=kOutput, calls=%fused_computation.7 | convolution fusion | flops 2013265920 | bytes 4063232 | tf_op jit(solution)/shard_map/dot_general | solution.py:41
  200.3 2.4 fusion.9
  202.7 2.4 fusion.11
  206.8 2.3 copy.111
  209.1 5.5 %pad_maximum_fusion = f32[2,1024,896]{2,1,0:T(8,128)} fusion(f32[2,1024,320]{2,1,0:T(8,128)S(1)} %copy.111, f32[2,1024,64]{2,1,0:T(8,128)} %copy.110, f32[2,1024,512]{2,1,0:T(8,128)} %all-gather.5.cloned.1.call-done), kind=kLoop, calls=%fused_computation.2 | loop fusion | flops 3670016 | bytes 14680064 | tf_op jit(solution)/shard_map/concatenate | solution.py:91
  214.6 7.1 %gather_fusion.1 = f32[8,2,128,896]{3,2,1,0:T(8,128)} fusion(f32[2,8,128,896]{3,2,1,0:T(8,128)} %bitcast.116, s32[1024]{0:T(1024)S(1)} %pad_clamp_fusion), kind=kCustom, calls=%fused_computation.1 | custom fusion | bytes 14680096 | tf_op jit(solution)/shard_map/jit(_take)/gather | solution.py:67
  221.7 3.8 %copy.112 = f32[2,8,128,896]{3,2,1,0:T(8,128)S(1)} copy(f32[2,8,128,896]{3,2,0,1:T(8,128)} %bitcast.115) | data formatting | bytes 14680064 | tf_op jit(solution)/shard_map/jit(_take)/gather | solution.py:67
  226.0 2.9 %copy-done.2 = f32[2,1024,896]{2,1,0:T(8,128)} copy-done((f32[2,1024,896]{2,1,0:T(8,128)}, f32[2,1024,896]{2,1,0:T(8,128)S(1)}, u32[]{:S(2)}) %copy-start.2) | copy-done | bytes 7340056
  231.1 3.9 %all-to-all-start.1 = ((f32[2,2,512,384]{3,2,1,0:T(8,128)}), f32[2,2,512,384]{3,2,1,0:T(8,128)S(1)}, u32[]{:S(2)}, u32[]{:S(2)}) async-start(f32[2,2,512,384]{3,2,1,0:T(8,128)} %copy.113), calls=%async_computation.1 | async-start | bytes 6291456 | tf_op jit(solution)/shard_map/all_to_all | solution.py:25
  235.2 2.2 slice-done
  238.1 25.5 %all-to-all-done.1 = f32[2,2,512,384]{3,2,1,0:T(8,128)S(1)} async-done(((f32[2,2,512,384]{3,2,1,0:T(8,128)}), f32[2,2,512,384]{3,2,1,0:T(8,128)S(1)}, u32[]{:S(2)}, u32[]{:S(2)}) %all-to-all-start.1) | async-done | bytes 3145760 | tf_op jit(solution)/shard_map/all_to_all | solution.py:25
  (59 shorter events, 25.8 us)
Async XLA Ops:
  7.2 79.9 %all-gather.3.cloned.1.call-start = ((), (), s32[]{:S(2)}) async-start(), calls=%async_computation.2 | async-start | bytes 2228224 | tf_op jit(solution)/shard_map/all_gather | solution.py:84
  7.9 170.8 %all-gather.5.cloned.1.call-start = ((), (), s32[]{:S(2)}) async-start(), calls=%async_computation.3 | async-start | bytes 4456448 | tf_op jit(solution)/shard_map/all_gather | solution.py:90
  7.9 15.8 %collective-permute-start = (f32[2,64,1024]{2,1,0:T(8,128)}, f32[2,64,1024]{2,1,0:T(8,128)S(1)}, u32[]{:S(2)}, u32[]{:S(2)}) collective-permute-start(f32[2,64,1024]{2,1,0:T(8,128)} %bitcast.121), channel_id=1, source_target_pairs={{0,16},{16,0},{1,17},{17,1},{2,18},{18,2},{3,19},{19,3},{4,20},{20... | collective-permute-start | bytes 1572872 | tf_op jit(solution)/shard_map/ppermute | solution.py:14
  87.1 4.8 %copy-start.3 = (f32[1,2,512,512]{2,3,1,0:T(8,128)S(1)}, f32[1,2,512,512]{2,3,1,0:T(8,128)}, u32[]{:S(2)}) copy-start(f32[1,2,512,512]{2,3,1,0:T(8,128)} %all-gather.3.cloned.1.call-done) | copy-start | bytes 6291460
  91.9 3.0 %copy-start.5 = (f32[1,2,64,1024]{3,2,1,0:T(8,128)S(1)}, f32[1,2,64,1024]{3,2,1,0:T(8,128)}, u32[]{:S(2)}) copy-start(f32[1,2,64,1024]{3,2,1,0:T(8,128)} %param.4) | copy-start | bytes 1572868
  95.0 10.5 %copy-start.6 = (s32[2,8]{1,0:T(2,128)S(1)}, s32[2,8]{1,0:T(2,128)}, u32[]{:S(2)}) copy-start(s32[2,8]{1,0:T(2,128)} %param.7) | copy-start | bytes 196
  97.5 32.6 %all-to-all-start = ((f32[16,1,8192]{2,1,0:T(1,128)}), f32[16,1,8192]{2,1,0:T(1,128)S(1)}, u32[]{:S(2)}, u32[]{:S(2)}) async-start(f32[16,1,8192]{2,1,0:T(1,128)} %reshape.137), calls=%async_computation | async-start | bytes 1048576 | tf_op jit(solution)/shard_map/all_to_all | solution.py:86
  178.7 7.6 %copy-start = (f32[2,1024,512]{2,1,0:T(8,128)S(1)}, f32[2,1024,512]{2,1,0:T(8,128)}, u32[]{:S(2)}) copy-start(f32[2,1024,512]{2,1,0:T(8,128)} %all-gather.5.cloned.1.call-done) | copy-start | bytes 12582916
  188.5 3.5 %copy-start.4 = (f32[2,512,320]{1,2,0:T(8,128)S(1)}, f32[2,512,320]{1,2,0:T(8,128)}, u32[]{:S(2)}) copy-start(f32[2,512,320]{1,2,0:T(8,128)} %param.6) | copy-start | bytes 3932164
  192.0 8.3 %copy-start.1 = (f32[2,1024,512]{2,1,0:T(8,128)S(1)}, f32[2,1024,512]{2,1,0:T(8,128)}, u32[]{:S(2)}) copy-start(f32[2,1024,512]{2,1,0:T(8,128)} %all-gather.5.cloned.1.call-done) | copy-start | bytes 12582916
  226.0 2.9 %copy-start.2 = (f32[2,1024,896]{2,1,0:T(8,128)}, f32[2,1024,896]{2,1,0:T(8,128)S(1)}, u32[]{:S(2)}) copy-start(f32[2,1024,896]{2,1,0:T(8,128)S(1)} %bitcast_select_fusion) | copy-start | bytes 22020100
  231.1 32.5 %all-to-all-start.1 = ((f32[2,2,512,384]{3,2,1,0:T(8,128)}), f32[2,2,512,384]{3,2,1,0:T(8,128)S(1)}, u32[]{:S(2)}, u32[]{:S(2)}) async-start(f32[2,2,512,384]{3,2,1,0:T(8,128)} %copy.113), calls=%async_computation.1 | async-start | bytes 6291456 | tf_op jit(solution)/shard_map/all_to_all | solution.py:25
  235.2 2.2 slice-start
Sparse Core Ops, SparseCore 0:
  10.1 76.9 all-gather.2
  95.0 83.6 all-gather.4
where the time goes:
time: 278 us; the launch traced here: 277 us
  waiting for transfers between devices  169 us (61%)
  local copies, waits for them, and re-layouts  32.3 us (12%)
  matrix products  32 us (12%)
  starting transfers between devices  15.5 us (6%)
  between operations  14.4 us (5%)
  other arithmetic  14.3 us (5%)
    all_gather x1, waiting for transfers between devices, per_device(): lax.all_gather(pivot_inverses, 'grp', axis=3, tiled=True)[0]  62.4 us
    all_gather x1, waiting for transfers between devices, per_device(): piece = lax.all_gather(raw_multipliers, 'grp', axis=1, tiled=True)  43.9 us
    dot_general x12, matrix products, product(): jnp.dot(first_part, second_part, precision=lax.Precision.HIGHEST, preferr...  32 us
    all_to_all x1, waiting for transfers between devices, summed_on_arrival(): lax.all_to_all(pieces, axis, split_axis=0, concat_axis=0, tiled=True)  25.5 us
    all_to_all x1, waiting for transfers between devices, per_device(): lax.all_to_all(beta_rows, 'grp', split_axis=2, concat_axis=1, tiled=True)  24.2 us
    ppermute x1, waiting for transfers between devices, partner(): return lax.ppermute(block, axis, route)  12.3 us
    gather x4, local copies, waits for them, and re-layouts, reorder(): return jnp.take(grouped, source, axis=1).reshape(matrix.shape)  11.5 us
    unnamed x18, local copies, waits for them, and re-layouts  8.03 us
  transfers between devices with their start and end apart: 5, of which 5 were waited for; matrix products, arithmetic and copies ran while one was open for 3% of the time, Pallas kernels for 0%

commit v1 on v0

--- a/solution.py
+++ b/solution.py
@@ -81,7 +81,10 @@
     to_beta, to_alpha = block_sources(face_blocks)
     panel_section = lax.dynamic_slice_in_dim(alpha_rows, sibling * panel_width, panel_width, 2)
     raw_multipliers = complex_dot(
-        panel_section, lax.all_gather(pivot_inverses, "grp", axis=3, tiled=True)[0]
+        panel_section,
+        jnp.concatenate(
+            lax.all_to_all(jnp.stack([pivot_inverses] * lax.axis_size("grp")), "grp", 0, 0), axis=3
+        )[0],
     )
     beta_cols = lax.all_to_all(beta_rows, "grp", split_axis=2, concat_axis=1, tiled=True)
     beta_perm = reorder(beta_cols, to_alpha)

time: 278 us -> 318 us (1.14)
  the two profiles are of different devices: /device:TPU:4 before, /device:TPU:22 now
where the time goes in v1:
time: 318 us; the launch traced here: 317 us
  waiting for transfers between devices  195 us (61%)
  local copies, waits for them, and re-layouts  35.2 us (11%)
  starting transfers between devices  30.1 us (9%)
  matrix products  29.5 us (9%)
  between operations  14.4 us (5%)
  other arithmetic  13.4 us (4%)
    all_to_all x1, waiting for transfers between devices, per_device(): lax.all_to_all(jnp.stack([pivot_inverses] * lax.axis_size('grp')), 'grp',...  80 us
    all_gather x1, waiting for transfers between devices, per_device(): piece = lax.all_gather(raw_multipliers, 'grp', axis=1, tiled=True)  43.2 us
    all_to_all x1, waiting for transfers between devices, per_device(): lax.all_to_all(beta_rows, 'grp', split_axis=2, concat_axis=1, tiled=True)  33.7 us
    dot_general x12, matrix products, product(): jnp.dot(first_part, second_part, precision=lax.Precision.HIGHEST, preferr...  29.5 us
    all_to_all x1, waiting for transfers between devices, summed_on_arrival(): lax.all_to_all(pieces, axis, split_axis=0, concat_axis=0, tiled=True)  25.8 us
    all_to_all x1, starting transfers between devices, per_device(): lax.all_to_all(jnp.stack([pivot_inverses] * lax.axis_size('grp')), 'grp',...  15.3 us
    ppermute x1, waiting for transfers between devices, partner(): return lax.ppermute(block, axis, route)  12.1 us
    gather x4, local copies, waits for them, and re-layouts, reorder(): return jnp.take(grouped, source, axis=1).reshape(matrix.shape)  11.5 us
  transfers between devices with their start and end apart: 5, of which 5 were waited for; matrix products, arithmetic and copies ran while one was open for 3% of the time, Pallas kernels for 0%

profile of v1, /device:TPU:22, one launch (start us, length us, event | category | flops | bytes accessed | tf_op | source)
XLA Modules:
  0.0 317.4 jit_solution(5088917410621433626)
XLA Ops:
  7.2 2.5 stack.26
  9.7 15.3 %all-to-all-start = ((f32[16,1,2,512,32]{3,4,2,1,0:T(8,128)}), f32[16,1,2,512,32]{3,4,2,1,0:T(8,128)S(1)}, u32[]{:S(2)}, u32[]{:S(2)}) async-start(f32[16,1,2,512,32]{3,4,2,1,0:T(8,128)} %stack.26), calls=%async_computation | async-start | bytes 4194304 | tf_op jit(solution)/shard_map/all_to_all | solution.py:86
  25.1 3.2 %collective-permute-start = (f32[2,64,1024]{2,1,0:T(8,128)S(1)}, f32[2,64,1024]{2,1,0:T(8,128)S(1)}, u32[]{:S(2)}, u32[]{:S(2)}) collective-permute-start(f32[2,64,1024]{2,1,0:T(8,128)S(1)} %bitcast.128), channel_id=1, source_target_pairs={{0,16},{16,0},{1,17},{17,1},{2,18},{18,2},{3,19},{19,3},{4,20},{20... | collective-permute-start | bytes 1572872 | tf_op jit(solution)/shard_map/ppermute | solution.py:14
  28.3 12.1 %collective-permute-done = f32[2,64,1024]{2,1,0:T(8,128)S(1)} collective-permute-done((f32[2,64,1024]{2,1,0:T(8,128)S(1)}, f32[2,64,1024]{2,1,0:T(8,128)S(1)}, u32[]{:S(2)}, u32[]{:S(2)}) %collective-permute-start) | collective-permute-done | bytes 524320 | tf_op jit(solution)/shard_map/ppermute | solution.py:14
  40.4 80.0 %all-to-all-done = f32[16,1,2,512,32]{3,4,2,1,0:T(8,128)S(1)} async-done(((f32[16,1,2,512,32]{3,4,2,1,0:T(8,128)}), f32[16,1,2,512,32]{3,4,2,1,0:T(8,128)S(1)}, u32[]{:S(2)}, u32[]{:S(2)}) %all-to-all-start) | async-done | bytes 2097184 | tf_op jit(solution)/shard_map/all_to_all | solution.py:86
  128.7 7.6 %all-to-all-start.1 = ((f32[16,1,8192]{2,1,0:T(1,128)}), f32[16,1,8192]{2,1,0:T(1,128)S(1)}, u32[]{:S(2)}, u32[]{:S(2)}) async-start(f32[16,1,8192]{2,1,0:T(1,128)} %reshape.144), calls=%async_computation.1 | async-start | bytes 1048576 | tf_op jit(solution)/shard_map/all_to_all | solution.py:89
  136.7 33.7 %all-to-all-done.1 = f32[16,1,8192]{2,1,0:T(1,128)S(1)} async-done(((f32[16,1,8192]{2,1,0:T(1,128)}), f32[16,1,8192]{2,1,0:T(1,128)S(1)}, u32[]{:S(2)}, u32[]{:S(2)}) %all-to-all-start.1) | async-done | bytes 524320 | tf_op jit(solution)/shard_map/all_to_all | solution.py:89
  175.2 43.2 %all-gather.2.cloned.1.call-done = f32[2,1024,512]{2,1,0:T(8,128)} async-done(((f32[2,64,512]{2,1,0:T(8,128)}), f32[2,1024,512]{2,1,0:T(8,128)}) %all-gather.2.cloned.1.call-update) | async-done | bytes 4194320 | tf_op jit(solution)/shard_map/all_gather | solution.py:93
  218.4 3.9 %fusion.3 = f32[1024,64]{0,1:T(8,128)S(1)} fusion(f32[2,1024,512]{2,1,0:T(8,128)} %all-gather.2.cloned.1.call-done, f32[2,512,64]{1,2,0:T(8,128)S(1)} %dynamic-slice_select_fusion), kind=kOutput, calls=%fused_computation.11 | convolution fusion | flops 402653184 | bytes 2490368 | tf_op jit(solution)/shard_map/dot_general | solution.py:41
  222.3 3.7 %fusion.2 = f32[1024,64]{0,1:T(8,128)S(1)} fusion(f32[2,1024,512]{2,1,0:T(8,128)} %all-gather.2.cloned.1.call-done, f32[2,512,64]{1,2,0:T(8,128)S(1)} %dynamic-slice_select_fusion), kind=kOutput, calls=%fused_computation.10 | convolution fusion | flops 402653184 | bytes 2490368 | tf_op jit(solution)/shard_map/dot_general | solution.py:41
  226.0 2.2 fusion.13
  228.2 2.2 fusion.15
  231.7 4.3 %fusion.1 = f32[1024,320]{0,1:T(8,128)S(1)} fusion(f32[2,1024,512]{2,1,0:T(8,128)} %all-gather.2.cloned.1.call-done, f32[2,512,320]{1,2,0:T(8,128)S(1)} %copy-done.3), kind=kOutput, calls=%fused_computation.9 | convolution fusion | flops 2013265920 | bytes 4063232 | tf_op jit(solution)/shard_map/dot_general | solution.py:41
  236.1 3.9 %fusion = f32[1024,320]{0,1:T(8,128)S(1)} fusion(f32[2,1024,512]{2,1,0:T(8,128)} %all-gather.2.cloned.1.call-done, f32[2,512,320]{1,2,0:T(8,128)S(1)} %copy-done.3), kind=kOutput, calls=%fused_computation.8 | convolution fusion | flops 2013265920 | bytes 4063232 | tf_op jit(solution)/shard_map/dot_general | solution.py:41
  240.0 2.4 fusion.9
  242.4 2.4 fusion.11
  246.5 2.3 copy.117
  248.8 5.5 %pad_maximum_fusion = f32[2,1024,896]{2,1,0:T(8,128)} fusion(f32[2,1024,320]{2,1,0:T(8,128)S(1)} %copy.117, f32[2,1024,64]{2,1,0:T(8,128)} %copy.116, f32[2,1024,512]{2,1,0:T(8,128)} %all-gather.2.cloned.1.call-done), kind=kLoop, calls=%fused_computation.2 | loop fusion | flops 3670016 | bytes 14680064 | tf_op jit(solution)/shard_map/concatenate | solution.py:94
  254.3 7.1 %gather_fusion.1 = f32[8,2,128,896]{3,2,1,0:T(8,128)} fusion(f32[2,8,128,896]{3,2,1,0:T(8,128)} %bitcast.118, s32[1024]{0:T(1024)S(1)} %pad_clamp_fusion), kind=kCustom, calls=%fused_computation.1 | custom fusion | bytes 14680096 | tf_op jit(solution)/shard_map/jit(_take)/gather | solution.py:67
  261.4 3.8 %copy.118 = f32[2,8,128,896]{3,2,1,0:T(8,128)S(1)} copy(f32[2,8,128,896]{3,2,0,1:T(8,128)} %bitcast.117) | data formatting | bytes 14680064 | tf_op jit(solution)/shard_map/jit(_take)/gather | solution.py:67
  265.8 2.9 copy-done.2
  270.8 3.9 %all-to-all-start.2 = ((f32[2,2,512,384]{3,2,1,0:T(8,128)}), f32[2,2,512,384]{3,2,1,0:T(8,128)S(1)}, u32[]{:S(2)}, u32[]{:S(2)}) async-start(f32[2,2,512,384]{3,2,1,0:T(8,128)} %copy.119), calls=%async_computation.2 | async-start | bytes 6291456 | tf_op jit(solution)/shard_map/all_to_all | solution.py:25
  274.9 2.2 slice-done
  277.8 25.8 %all-to-all-done.2 = f32[2,2,512,384]{3,2,1,0:T(8,128)S(1)} async-done(((f32[2,2,512,384]{3,2,1,0:T(8,128)}), f32[2,2,512,384]{3,2,1,0:T(8,128)S(1)}, u32[]{:S(2)}, u32[]{:S(2)}) %all-to-all-start.2) | async-done | bytes 3145760 | tf_op jit(solution)/shard_map/all_to_all | solution.py:25
  (59 shorter events, 26.9 us)
Async XLA Ops:
  9.7 15.4 %copy-start.4 = (f32[1,2,64,1024]{3,2,1,0:T(8,128)S(1)}, f32[1,2,64,1024]{3,2,1,0:T(8,128)}, u32[]{:S(2)}) copy-start(f32[1,2,64,1024]{3,2,1,0:T(8,128)} %param.4) | copy-start | bytes 1572868
  9.7 110.7 %all-to-all-start = ((f32[16,1,2,512,32]{3,4,2,1,0:T(8,128)}), f32[16,1,2,512,32]{3,4,2,1,0:T(8,128)S(1)}, u32[]{:S(2)}, u32[]{:S(2)}) async-start(f32[16,1,2,512,32]{3,4,2,1,0:T(8,128)} %stack.26), calls=%async_computation | async-start | bytes 4194304 | tf_op jit(solution)/shard_map/all_to_all | solution.py:86
  25.0 193.4 %all-gather.2.cloned.1.call-start = ((), (), s32[]{:S(2)}) async-start(), calls=%async_computation.3 | async-start | bytes 4456448 | tf_op jit(solution)/shard_map/all_gather | solution.py:93
  25.1 15.3 %collective-permute-start = (f32[2,64,1024]{2,1,0:T(8,128)S(1)}, f32[2,64,1024]{2,1,0:T(8,128)S(1)}, u32[]{:S(2)}, u32[]{:S(2)}) collective-permute-start(f32[2,64,1024]{2,1,0:T(8,128)S(1)} %bitcast.128), channel_id=1, source_target_pairs={{0,16},{16,0},{1,17},{17,1},{2,18},{18,2},{3,19},{19,3},{4,20},{20... | collective-permute-start | bytes 1572872 | tf_op jit(solution)/shard_map/ppermute | solution.py:14
  126.2 10.1 %copy-start.5 = (s32[2,8]{1,0:T(2,128)S(1)}, s32[2,8]{1,0:T(2,128)}, u32[]{:S(2)}) copy-start(s32[2,8]{1,0:T(2,128)} %param.7) | copy-start | bytes 196
  128.7 41.8 %all-to-all-start.1 = ((f32[16,1,8192]{2,1,0:T(1,128)}), f32[16,1,8192]{2,1,0:T(1,128)S(1)}, u32[]{:S(2)}, u32[]{:S(2)}) async-start(f32[16,1,8192]{2,1,0:T(1,128)} %reshape.144), calls=%async_computation.1 | async-start | bytes 1048576 | tf_op jit(solution)/shard_map/all_to_all | solution.py:89
  218.4 7.6 %copy-start = (f32[2,1024,512]{2,1,0:T(8,128)S(1)}, f32[2,1024,512]{2,1,0:T(8,128)}, u32[]{:S(2)}) copy-start(f32[2,1024,512]{2,1,0:T(8,128)} %all-gather.2.cloned.1.call-done) | copy-start | bytes 12582916
  228.2 3.5 %copy-start.3 = (f32[2,512,320]{1,2,0:T(8,128)S(1)}, f32[2,512,320]{1,2,0:T(8,128)}, u32[]{:S(2)}) copy-start(f32[2,512,320]{1,2,0:T(8,128)} %param.6) | copy-start | bytes 3932164
  231.7 8.3 %copy-start.1 = (f32[2,1024,512]{2,1,0:T(8,128)S(1)}, f32[2,1024,512]{2,1,0:T(8,128)}, u32[]{:S(2)}) copy-start(f32[2,1024,512]{2,1,0:T(8,128)} %all-gather.2.cloned.1.call-done) | copy-start | bytes 12582916
  265.8 2.9 copy-start.2
  270.8 32.8 %all-to-all-start.2 = ((f32[2,2,512,384]{3,2,1,0:T(8,128)}), f32[2,2,512,384]{3,2,1,0:T(8,128)S(1)}, u32[]{:S(2)}, u32[]{:S(2)}) async-start(f32[2,2,512,384]{3,2,1,0:T(8,128)} %copy.119), calls=%async_computation.2 | async-start | bytes 6291456 | tf_op jit(solution)/shard_map/all_to_all | solution.py:25
  274.9 2.2 slice-start
Sparse Core Ops, SparseCore 0:
  126.3 92.1 all-gather.1
